TPU v7x, 32 devices: a 4x4x1 block of a 4x4x8 slice. The times are simulated.
32 devices in a mesh: data: 1 (over z), seq: 32 (over y, x, core).
Axes of the slice: x: 4, y: 4, z: 1, core: 2. Of those that a mesh axis runs over, the one named last changes fastest.
The devices are a block of a 4x4x8 slice.
Arguments:
- x: bfloat16 [8192, 4096], P(('data', 'seq'))
- g: float32 [4096], replicated
- wqkv: bfloat16 [4096, 3, 32, 128], replicated
- wo: bfloat16 [32, 128, 4096], replicated
Outputs:
- output: bfloat16 [8192, 4096], P(('data', 'seq'))
All inputs are finite; a program needn't handle non-finite values.
Results may differ from a plain program's by a relative error of at most 0.0030117.
Values are sent between devices in bfloat16 or wider.
A program may use at most 768 MiB of HBM per device.

v0:
```python
import jax
import jax.numpy as jnp
from jax import lax
from jax.sharding import PartitionSpec as P


def _angles(pos, dh):
    half = dh // 2
    inv = 10000.0 ** (-jnp.arange(half, dtype=jnp.float32) * 2.0 / dh)
    ang = pos[:, None] * inv[None, :]
    return jnp.cos(ang)[:, None, :], jnp.sin(ang)[:, None, :]


def _rope(x, cos, sin):
    half = x.shape[-1] // 2
    x1, x2 = x[..., :half], x[..., half:]
    return jnp.concatenate([x1 * cos - x2 * sin, x2 * cos + x1 * sin], axis=-1)


def solution(mesh):
    p = mesh.shape["seq"]
    rows = P(("data", "seq"), None)

    def local(x, g, wqkv, wo):
        t, d = x.shape
        _, _, h, dh = wqkv.shape
        me = lax.axis_index("seq")
        xf = x.astype(jnp.float32)
        xn = (xf * lax.rsqrt(jnp.mean(xf * xf, axis=-1, keepdims=True) + 1e-5) * g).astype(jnp.bfloat16)
        qkv = jnp.einsum("td,dchk->cthk", xn, wqkv, preferred_element_type=jnp.float32)
        pos = (me * t + jnp.arange(t)).astype(jnp.float32)
        cos, sin = _angles(pos, dh)
        buf = jnp.concatenate([_rope(qkv[:2], cos, sin), qkv[2:]], axis=0).astype(jnp.bfloat16)
        buf = lax.all_to_all(buf, "seq", 2, 1, tiled=True)
        qkv_h = buf.transpose(0, 2, 1, 3)
        q, k, v = qkv_h[0], qkv_h[1], qkv_h[2]
        scale = dh ** -0.5
        outs = []
        for j in range(p):
            lo, hi = j * t, (j + 1) * t
            sc = jnp.einsum("hqd,hkd->hqk", q[:, lo:hi], k[:, :hi], preferred_element_type=jnp.float32) * scale
            mask = (lo + jnp.arange(t))[:, None] >= jnp.arange(hi)[None, :]
            sc = jnp.where(mask, sc, -jnp.inf)
            pr = jax.nn.softmax(sc, axis=-1).astype(jnp.bfloat16)
            outs.append(jnp.einsum("hqk,hkd->hqd", pr, v[:, :hi], preferred_element_type=jnp.float32).astype(jnp.bfloat16))
        o = jnp.concatenate(outs, axis=1).transpose(1, 0, 2)
        o = lax.all_to_all(o, "seq", 0, 1, tiled=True)
        y = xf + jnp.einsum("thk,hkd->td", o, wo, preferred_element_type=jnp.float32)
        return y.astype(jnp.bfloat16)

    return jax.shard_map(local, mesh=mesh,
                         in_specs=(rows, P(None), P(None, None, None, None), P(None, None, None)),
                         out_specs=rows, check_vma=False)
```

profile of v0, /device:TPU:97, one launch (start us, length us, event | category | flops | bytes accessed | tf_op | source)
XLA Modules:
  0.0 544.1 jit_solution(6501050748741957404)
XLA Ops:
  0.0 122.6 %copy.16 = bf16[4096,3,32,128]{0,3,2,1:T(8,128)(2,1)} copy(bf16[4096,3,32,128]{3,2,1,0:T(8,128)(2,1)} %param.6) | data formatting | bytes 201326592 | tf_op args[2]
  123.2 38.0 %fusion.71 = f32[256,12288]{0,1:S(1)} fusion(bf16[4096,12288]{0,1:T(8,128)(2,1)} %bitcast, bf16[256,4096]{1,0:T(8,128)(2,1)} %param.4, f32[4096]{0:T(1024)S(1)} %copy-done.22, f32[256]{0:T(256)S(1)} %add_rsqrt_fusion), kind=kOutput, calls=%fused_computation.179 | convolution fusion | flops 25773998080 | bytes 115360768
  166.9 9.1 %all-to-all-start = ((bf16[3,256,32,128]{1,3,0,2:T(8,128)(2,1)}), bf16[3,256,32,128]{1,3,0,2:T(8,128)(2,1)}, u32[]{:S(2)}, u32[]{:S(2)}) async-start(bf16[3,256,32,128]{1,3,0,2:T(8,128)(2,1)} %copy.17), calls=%async_computation | async-start | bytes 12582912 | tf_op jit(solution)/shard_map/all_to_all | solution.py:34
  176.9 76.5 %all-to-all-done = bf16[3,256,32,128]{1,3,0,2:T(8,128)(2,1)} async-done(((bf16[3,256,32,128]{1,3,0,2:T(8,128)(2,1)}), bf16[3,256,32,128]{1,3,0,2:T(8,128)(2,1)}, u32[]{:S(2)}, u32[]{:S(2)}) %all-to-all-start) | async-done | bytes 6291488 | tf_op jit(solution)/shard_map/all_to_all | solution.py:34
  253.4 9.1 %copy.18 = bf16[3,256,32,128]{3,1,2,0:T(8,128)(2,1)} copy(bf16[3,256,32,128]{1,3,0,2:T(8,128)(2,1)} %all-to-all-done) | data formatting | bytes 12582912 | tf_op jit(solution)/shard_map/all_to_all | solution.py:34
  262.5 5.0 fusion.196
  302.6 3.6 fusion.216
  306.2 3.5 fusion.217
  317.8 6.4 %fusion.223 = (f32[256]{0:T(256)}, f32[256,6912]{1,0:T(8,128)}) fusion(bf16[1,8192,128]{2,1,0:T(8,128)(2,1)} %bitcast.722, bf16[1,8192,128]{2,1,0:T(8,128)(2,1)} %bitcast.754, s32[256]{0:T(256)S(1)} %iota_add_fusion.5), kind=kOutput, calls=%fused_computation.496 | convolution fusion | flops 460062464 | bytes 8914944 | tf_op jit(solution)/shard_map/hqd,hkd->hqk/dot_general | solution.py:41
  324.1 6.5 %fusion.224 = (f32[256]{0:T(256)}, f32[256,7168]{1,0:T(8,128)}) fusion(bf16[1,8192,128]{2,1,0:T(8,128)(2,1)} %bitcast.723, bf16[1,8192,128]{2,1,0:T(8,128)(2,1)} %bitcast.755, s32[256]{0:T(256)S(1)} %iota_add_fusion.4), kind=kOutput, calls=%fused_computation.497 | convolution fusion | flops 477101824 | bytes 9242624 | tf_op jit(solution)/shard_map/hqd,hkd->hqk/dot_general | solution.py:41
  330.6 6.6 %fusion.225 = (f32[256]{0:T(256)}, f32[256,7424]{1,0:T(8,128)}) fusion(bf16[1,8192,128]{2,1,0:T(8,128)(2,1)} %bitcast.724, bf16[1,8192,128]{2,1,0:T(8,128)(2,1)} %bitcast.756, s32[256]{0:T(256)S(1)} %iota_add_fusion.3), kind=kOutput, calls=%fused_computation.498 | convolution fusion | flops 494141184 | bytes 9570304 | tf_op jit(solution)/shard_map/hqd,hkd->hqk/dot_general | solution.py:41
  337.2 6.8 %fusion.226 = (f32[256]{0:T(256)}, f32[256,7680]{1,0:T(8,128)}) fusion(bf16[1,8192,128]{2,1,0:T(8,128)(2,1)} %bitcast.725, bf16[1,8192,128]{2,1,0:T(8,128)(2,1)} %bitcast.757, s32[256]{0:T(256)S(1)} %iota_add_fusion.2), kind=kOutput, calls=%fused_computation.499 | convolution fusion | flops 511180544 | bytes 9897984 | tf_op jit(solution)/shard_map/hqd,hkd->hqk/dot_general | solution.py:41
  344.1 6.8 %fusion.227 = (f32[256]{0:T(256)}, f32[256,7936]{1,0:T(8,128)}) fusion(bf16[1,8192,128]{2,1,0:T(8,128)(2,1)} %bitcast.726, bf16[1,8192,128]{2,1,0:T(8,128)(2,1)} %bitcast.758, s32[256]{0:T(256)S(1)} %iota_add_fusion.1), kind=kOutput, calls=%fused_computation.500 | convolution fusion | flops 528219904 | bytes 10225664 | tf_op jit(solution)/shard_map/hqd,hkd->hqk/dot_general | solution.py:41
  381.9 3.6 fusion.161
  388.2 3.6 fusion.159
  394.8 3.8 fusion.157
  401.6 3.9 fusion.155
  411.2 4.1 fusion.153
  418.7 4.5 fusion.151
  426.6 4.4 fusion.149
  472.3 3.9 reduce.128
  478.2 40.6 %all_to_all.33 = bf16[32,2,16384]{2,1,0:T(2,128)(2,1)S(1)} all-to-all(bf16[32,2,16384]{2,1,0:T(2,128)(2,1)} %reshape.1265), channel_id=1, replica_groups=mesh['data'=1,'seq'=32] {'seq'}, dimensions={0} | all-to-all | bytes 4194304 | tf_op jit(solution)/shard_map/all_to_all | solution.py:47
  518.8 6.8 %reshape.1266 = bf16[8192,1,128]{2,1,0:T(2,128)(2,1)} reshape(bf16[32,2,16384]{2,1,0:T(2,128)(2,1)S(1)} %all_to_all.33) | data formatting | bytes 4194304
  528.4 15.5 %fusion.30 = bf16[256,4096]{1,0:T(8,128)(2,1)} fusion(bf16[256,32,128]{2,0,1:T(8,128)(2,1)S(1)} %bitcast.662, bf16[32,128,4096]{2,1,0:T(8,128)(2,1)} %param.7, bf16[256,4096]{1,0:T(8,128)(2,1)S(1)} %copy-done.5), kind=kOutput, calls=%fused_computation.94 | convolution fusion | flops 8593080320 | bytes 39845888 | tf_op jit(solution)/shard_map/thk,hkd->td/dot_general | solution.py:48
  (198 shorter events, 148.3 us)
Async XLA Ops:
  0.0 122.6 %copy-start.4 = (bf16[256,4096]{1,0:T(8,128)(2,1)S(1)}, bf16[256,4096]{1,0:T(8,128)(2,1)}, u32[]{:S(2)}) copy-start(bf16[256,4096]{1,0:T(8,128)(2,1)} %param.4) | copy-start | bytes 6291460
  0.0 123.1 %copy-start.22 = (f32[4096]{0:T(1024)S(1)}, f32[4096]{0:T(1024)}, u32[]{:S(2)}) copy-start(f32[4096]{0:T(1024)} %param.5) | copy-start | bytes 49156
  166.9 86.5 %all-to-all-start = ((bf16[3,256,32,128]{1,3,0,2:T(8,128)(2,1)}), bf16[3,256,32,128]{1,3,0,2:T(8,128)(2,1)}, u32[]{:S(2)}, u32[]{:S(2)}) async-start(bf16[3,256,32,128]{1,3,0,2:T(8,128)(2,1)} %copy.17), calls=%async_computation | async-start | bytes 12582912 | tf_op jit(solution)/shard_map/all_to_all | solution.py:34
  267.5 46.0 %copy-start.9 = (bf16[1,32,256,1,128]{4,2,1,3,0:T(8,128)(2,1)}, bf16[1,32,256,1,128]{4,2,1,3,0:T(8,128)(2,1)S(1)}, u32[]{:S(2)}) copy-start(bf16[1,32,256,1,128]{4,2,1,3,0:T(8,128)(2,1)S(1)} %get-tuple-element.8) | copy-start | bytes 6291460
  267.5 46.0 %copy-start.11 = (bf16[1,32,256,1,128]{4,2,1,3,0:T(8,128)(2,1)}, bf16[1,32,256,1,128]{4,2,1,3,0:T(8,128)(2,1)S(1)}, u32[]{:S(2)}) copy-start(bf16[1,32,256,1,128]{4,2,1,3,0:T(8,128)(2,1)S(1)} %get-tuple-element.9) | copy-start | bytes 6291460
  350.8 6.3 %copy-start.16 = (f32[256,768]{1,0:T(8,128)S(1)}, f32[256,768]{1,0:T(8,128)}, u32[]{:S(2)}) copy-start(f32[256,768]{1,0:T(8,128)} %get-tuple-element.17) | copy-start | bytes 2359300
  351.9 5.5 %copy-start.6 = (bf16[1,32,256,1,128]{4,2,1,3,0:T(8,128)(2,1)S(1)}, bf16[1,32,256,1,128]{4,2,1,3,0:T(8,128)(2,1)}, u32[]{:S(2)}) copy-start(bf16[1,32,256,1,128]{4,2,1,3,0:T(8,128)(2,1)} %get-tuple-element.7) | copy-start | bytes 6291460
  443.2 3.8 slice-start.8
  444.8 2.3 slice-start.9
  444.8 2.3 copy-start.21
  447.1 3.4 slice-start.6
  448.2 2.3 slice-start.7
  450.5 3.5 slice-start.4
  451.7 2.3 slice-start.5
  451.7 2.3 copy-start.19
  454.0 3.6 slice-start.2
  455.3 2.3 slice-start.3
  455.3 2.3 copy-start.18
  457.6 3.9 slice-start
  458.9 2.6 slice-start.1
  458.9 2.6 copy-start.17
  462.8 2.4 copy-start.10
  462.9 2.4 copy-start.23
  525.6 2.9 copy-start.5
  (11 other events, 18.4 us)
where the time goes:
time: 555 us; the launch traced here: 544 us
  matrix products  212 us (38%)
  local copies, waits for them, and re-layouts  156 us (28%)
  waiting for transfers between devices  76.5 us (14%)
  other arithmetic  49.5 us (9%)
  blocking collectives  40.6 us (7%)
  starting transfers between devices  9.14 us (2%)
    unnamed x72, local copies, waits for them, and re-layouts  138 us
    dot_general x32, matrix products, local(): jnp.einsum('hqd,hkd->hqk', q[:, lo:hi], k[:, :hi], preferred_element_type...  85.8 us
    all_to_all x1, waiting for transfers between devices, local(): buf = lax.all_to_all(buf, 'seq', 2, 1, tiled=True)  76.5 us
    dot_general x32, matrix products, local(): jnp.einsum('hqk,hkd->hqd', pr, v[:, :hi], preferred_element_type=jnp.floa...  72.4 us
    reduce_sum x32, other arithmetic, local(): pr = jax.nn.softmax(sc, axis=-1).astype(jnp.bfloat16)  42.2 us
    all_to_all x1, blocking collectives, local(): o = lax.all_to_all(o, 'seq', 0, 1, tiled=True)  40.6 us
    unnamed x1, matrix products  38 us
    dot_general x1, matrix products, local(): jnp.einsum('thk,hkd->td', o, wo, preferred_element_type=jnp.float32)  15.5 us
  transfers between devices with their start and end apart: 1, of which 1 were waited for; matrix products, arithmetic and copies ran while one was open for 0% of the time, Pallas kernels for 0%

commit v1 on v0

v1 whole, which is shorter than its diff:
```python
import functools
import math

import jax
import jax.numpy as jnp
from jax import lax
from jax.experimental import pallas as pl
from jax.experimental.pallas import tpu as pltpu
from jax.sharding import PartitionSpec as P

BF = jnp.bfloat16
F32 = jnp.float32
MESH = pl.DeviceIdType.MESH


def _place(n):
    me = lax.axis_index("seq")
    core = lax.rem(me, 2)
    x = lax.rem(me // 2, n)
    y = me // (2 * n)
    return y, x, core, (lambda yy, xx, cc: {"seq": (yy * n + xx) * 2 + cc})


def _qkv_kernel(n, nc, ahead, x_ref, g_ref, cos_ref, sin_ref, w_ref, out_ref,
                xg, wst, wf, w, yst, rb, wsem, xs_s, xs_r, rl_s, ys_s, ys_r, rb_s, rb_r, fw_s, loc_s):
    t, d = x_ref.shape
    r = t // nc
    dk = wst.shape[1]
    y, x, core, dev = _place(n)
    step_x = 1 - 2 * core
    xf_, xb_ = lax.rem(x + step_x + n, n), lax.rem(x - step_x + n, n)
    yf_, yb_ = lax.rem(y + step_x + n, n), lax.rem(y - step_x + n, n)
    xo = lax.rem(x + 2, n)
    xslot = (x, xb_, xf_, xo)
    yd = [lax.rem(y + k, n) for k in range(n)]

    barrier = pltpu.get_barrier_semaphore()
    peers = [dev(y, xf_, core), dev(y, xb_, core), dev(y, x, 1 - core)]
    peers += [dev(yd[k], x, cc) for k in (1, n - 1) for cc in (0, 1)]
    for p_ in peers:
        pl.semaphore_signal(barrier, inc=1, device_id=p_, device_id_type=MESH)

    hb = x * (2 * n)

    def wload(i):
        return pltpu.make_async_copy(
            w_ref.at[pl.ds(pl.multiple_of(i * dk, dk), dk), :, pl.ds(pl.multiple_of(hb, 2 * n), 2 * n), :],
            wst.at[lax.rem(i, 2)], wsem.at[lax.rem(i, 2)])

    wload(0).start()
    wload(1).start()

    def norm(j, _):
        xv = x_ref[pl.ds(pl.multiple_of(j * r, r), r), :].astype(F32)
        v = xv * lax.rsqrt(jnp.mean(xv * xv, axis=-1, keepdims=True) + 1e-5) * g_ref[...]
        xg[j, 0] = v.astype(BF)
        return 0

    lax.fori_loop(0, nc, norm, 0)
    pl.semaphore_wait(barrier, len(peers))

    def own(j, k):
        return pltpu.make_async_remote_copy(
            xg.at[j, 0], xg.at[j, 1 + k], xs_s.at[k, j], xs_r.at[k, j],
            device_id=dev(y, (xf_, xb_)[k], core), device_id_type=MESH)

    def relay(j):
        return pltpu.make_async_remote_copy(
            xg.at[j, 1], xg.at[j, 3], rl_s.at[j], xs_r.at[2, j],
            device_id=dev(y, xf_, core), device_id_type=MESH)

    for j in range(ahead):
        own(j, 0).start()
        own(j, 1).start()

    nw = d // dk
    sub = wf.shape[1] // (2 * n)

    def relayout(i, _):
        wload(i).wait()
        slot = lax.rem(i, 2)
        for s in range(dk // sub):
            for c in range(3):
                b = (s * 3 + c) % 2
                wf[b] = wst[slot, s * sub:(s + 1) * sub, c, :, :].astype(F32).reshape(sub * 2 * n, 128)
                for h in range(2 * n):
                    rows = wf[b, pl.ds(h, sub, stride=2 * n), :]
                    w[h // 2, pl.ds(pl.multiple_of(i * dk + s * sub, sub), sub),
                      ((h % 2) * 3 + c) * 128:((h % 2) * 3 + c + 1) * 128] = rows.astype(BF)

        @pl.when(i + 2 < nw)
        def _():
            wload(i + 2).start()

        @pl.when(i == nw // 2)
        def _():
            own(0, 0).wait_recv()
            relay(0).start()
        return 0

    lax.fori_loop(0, nw, relayout, 0)

    def near(j, k, cc):
        return pltpu.make_async_remote_copy(
            yst.at[j, k, cc], out_ref.at[:, y, :, core, j], ys_s.at[k, cc, j], ys_r.at[k, core, j],
            device_id=dev(yd[k], x, cc), device_id_type=MESH)

    def sibling(j):
        return pltpu.make_async_remote_copy(
            yst.at[j, 0, 1 - core], out_ref.at[:, y, :, core, j], ys_s.at[0, 1, j], ys_r.at[0, core, j],
            device_id=dev(y, x, 1 - core), device_id_type=MESH)

    def local(j):
        return pltpu.make_async_copy(yst.at[j, 0, core], out_ref.at[:, y, :, core, j], loc_s.at[j])

    def hop(j):
        return pltpu.make_async_remote_copy(
            yst.at[j, 2], rb.at[j], rb_s.at[j], rb_r.at[j],
            device_id=dev(yf_, x, core), device_id_type=MESH)

    def forward(j, cc):
        return pltpu.make_async_remote_copy(
            rb.at[j, cc], out_ref.at[:, yb_, :, core, j], fw_s.at[cc, j], ys_r.at[2, core, j],
            device_id=dev(yf_, x, cc), device_id_type=MESH)

    def step(j, _):
        @pl.when(j + ahead < nc)
        def _():
            own(j + ahead, 0).start()
            own(j + ahead, 1).start()

        @pl.when(j + 1 < nc)
        def _():
            own(j + 1, 0).wait_recv()
            relay(j + 1).start()

        @pl.when(j >= 1)
        def _():
            hop(j - 1).wait_recv()
            forward(j - 1, 0).start()
            forward(j - 1, 1).start()

        own(j, 1).wait_recv()
        relay(j).wait_recv()
        lhs = xg[j].reshape(4 * r, d)
        cosv = jnp.concatenate([cos_ref[xs, j] for xs in xslot], axis=0)
        sinv = jnp.concatenate([sin_ref[xs, j] for xs in xslot], axis=0)
        for k in (2, 1, 3, 0):
            acc = jnp.dot(lhs, w[yd[k]], preferred_element_type=F32)
            for cc in range(2):
                for c in range(3):
                    v = acc[:, (cc * 3 + c) * 128:(cc * 3 + c + 1) * 128]
                    if c < 2:
                        v = v * cosv + pltpu.roll(v, 64, 1) * sinv
                    v = v.astype(BF)
                    for s in range(4):
                        yst[j, k, cc, c, xslot[s]] = v[s * r:(s + 1) * r]
            if k == 2:
                hop(j).start()
            elif k == 0:
                sibling(j).start()
                local(j).start()
            else:
                near(j, k, 0).start()
                near(j, k, 1).start()
        return 0

    lax.fori_loop(0, nc, step, 0)
    hop(nc - 1).wait_recv()
    forward(nc - 1, 0).start()
    forward(nc - 1, 1).start()

    def drain(j, _):
        for k in range(2):
            own(j, k).wait_send()
        relay(j).wait_send()
        hop(j).wait_send()
        for cc in range(2):
            forward(j, cc).wait_send()
            for k in (1, 3):
                near(j, k, cc).wait_send()
        sibling(j).wait_send()
        local(j).wait()
        for k in (1, 2, 3):
            for cc in range(2):
                pltpu.make_async_remote_copy(
                    yst.at[j, k, cc], out_ref.at[:, yd[n - k], :, cc, j], ys_s.at[k, cc, j], ys_r.at[k, cc, j],
                    device_id=dev(y, x, 1 - core), device_id_type=MESH).wait_recv()
        pltpu.make_async_remote_copy(
            yst.at[j, 0, core], out_ref.at[:, y, :, 1 - core, j], ys_s.at[0, 1, j], ys_r.at[0, 1 - core, j],
            device_id=dev(y, x, 1 - core), device_id_type=MESH).wait_recv()
        return 0

    lax.fori_loop(0, nc, drain, 0)


def qkv_exchange(n, nc, ahead, x, g, cos, sin, wqkv):
    t, d = x.shape
    h, dh = wqkv.shape[2:]
    r = t // nc
    dk = 128
    vm = pl.BlockSpec(memory_space=pltpu.VMEM)
    dma = pltpu.SemaphoreType.DMA
    return pl.pallas_call(
        functools.partial(_qkv_kernel, n, nc, ahead),
        out_shape=jax.ShapeDtypeStruct((3, n, n, 2, nc, r, dh), BF),
        in_specs=[vm, vm, vm, vm, pl.BlockSpec(memory_space=pl.ANY)],
        out_specs=pl.BlockSpec(memory_space=pl.ANY),
        scratch_shapes=[
            pltpu.VMEM((nc, 4, r, d), BF),
            pltpu.VMEM((2, dk, 3, 2 * n, dh), BF),
            pltpu.VMEM((2, 32 * 2 * n, dh), F32),
            pltpu.VMEM((n, d, 6 * dh), BF),
            pltpu.VMEM((nc, n, 2, 3, n, r, dh), BF),
            pltpu.VMEM((nc, 2, 3, n, r, dh), BF),
            dma((2,)), dma((2, nc)), dma((3, nc)), dma((nc,)),
            dma((n, 2, nc)), dma((n, 2, nc)), dma((nc,)), dma((nc,)), dma((2, nc)), dma((nc,)),
        ],
        compiler_params=pltpu.CompilerParams(collective_id=0, has_side_effects=True, vmem_limit_bytes=64 * 2**20 - 2**16),
        cost_estimate=pl.CostEstimate(flops=2 * t * d * 3 * h * dh, bytes_accessed=40 * 2**20, transcendentals=0),
    )(x, g.reshape(1, d), cos, sin, wqkv)


def tables(n, t, dh, nc):
    y, x, core, _ = _place(n)
    pos = (((y * n + jnp.arange(n))[:, None] * 2 + core) * t + jnp.arange(t)[None, :]).astype(F32)
    inv = 10000.0 ** (-jnp.arange(dh // 2, dtype=F32) * 2.0 / dh)
    ang = pos[..., None] * inv
    cos, sin = jnp.cos(ang), jnp.sin(ang)
    shape = (n, nc, t // nc, dh)
    return jnp.concatenate([cos, cos], -1).reshape(shape), jnp.concatenate([-sin, sin], -1).reshape(shape)


NEG = -1e30

def flash_kernel(q_ref, k_ref, v_ref, o_ref, vt_ref, qt_ref, s_ref, acc_ref, m_ref, l_ref, *, bq, bk, qt, sub, mxl, pre):
    i = pl.program_id(0)
    S, d = k_ref.shape
    c = (d ** -0.5) * math.log2(math.e)
    dv = vt_ref.shape[0]

    @pl.when(i == 0)
    def _():
        if mxl:
            vt_ref[d:, :] = jnp.ones((dv - d, S), jnp.bfloat16)
        def tr(j, _):
            blk = pl.ds(pl.multiple_of(j * 512, 512), 512)
            vt_ref[0:d, blk] = v_ref[blk, :].T
            return 0
        lax.fori_loop(0, S // 512, tr, 0)
    if pre:
        qt_ref[...] = q_ref[...].T
    acc_ref[...] = jnp.zeros_like(acc_ref)
    m_ref[...] = jnp.full_like(m_ref, NEG)
    l_ref[...] = jnp.zeros_like(l_ref)

    def block(k0, n, masked):
        for t in range(bq // qt):
            cols = slice(t * qt, (t + 1) * qt)
            if masked:
                nn = min(n, (t + 1) * qt)
            else:
                nn = n
            m_old = m_ref[:, cols]
            m_new = m_old
            ss = []
            step = min(nn, 512)
            for u in range(nn // step):
                ks = pl.ds(pl.multiple_of(k0 + u * step, step), step)
                if pre:
                    s = jnp.dot(k_ref[ks, :], qt_ref[:, cols], preferred_element_type=jnp.float32)
                else:
                    s = lax.dot_general(k_ref[ks, :], q_ref[cols, :], (((1,), (1,)), ((), ())), preferred_element_type=jnp.float32)
                if masked:
                    kp = lax.broadcasted_iota(jnp.int32, s.shape, 0) + u * step
                    qp = lax.broadcasted_iota(jnp.int32, s.shape, 1) + t * qt
                    s = jnp.where(kp <= qp, s, NEG)
                s_ref[t % 2, u * step:(u + 1) * step, :] = s
                m_new = jnp.maximum(m_new, jnp.max(s, axis=0, keepdims=True))
            a = jnp.exp2((m_old - m_new) * c)
            mc = m_new * c
            l = l_ref[:, cols] * a
            acc = acc_ref[:, cols] * a
            part = None
            for u in range(nn // sub):
                ks = pl.ds(pl.multiple_of(k0 + u * sub, sub), sub)
                p = jnp.exp2(s_ref[t % 2, u * sub:(u + 1) * sub, :] * c - mc)
                if not mxl:
                    l = l + jnp.sum(p, axis=0, keepdims=True)
                dd = jnp.dot(vt_ref[:, ks], p.astype(jnp.bfloat16), preferred_element_type=jnp.float32)
                part = dd if part is None else part + dd
            m_ref[:, cols] = m_new
            l_ref[:, cols] = l
            acc_ref[:, cols] = acc + part

    nfull = (i * bq) // bk
    lax.fori_loop(0, nfull, lambda j, _: (block(j * bk, bk, False), 0)[1], 0)
    rest0 = nfull * bk
    if bk > bq:
        nrest = (i * bq - rest0) // bq
        lax.fori_loop(0, nrest, lambda j, _: (block(rest0 + j * bq, bq, False), 0)[1], 0)
    block(i * bq, bq, True)
    l = acc_ref[d:d + 1, :] if mxl else l_ref[...]
    o = acc_ref[0:d, :] * (1.0 / l)
    o_ref[...] = o.T.astype(o_ref.dtype)

def flash(q, k, v, bq=512, bk=2048, qt=512, sub=256, mxl=0, pre=1):
    S, d = q.shape
    dv = d + 16 * mxl
    whole = pl.BlockSpec((S, d), lambda i: (0, 0))
    return pl.pallas_call(
        functools.partial(flash_kernel, bq=bq, bk=bk, qt=qt, sub=sub, mxl=mxl, pre=pre),
        out_shape=jax.ShapeDtypeStruct((S, d), jnp.bfloat16),
        grid=(S // bq,),
        in_specs=[pl.BlockSpec((bq, d), lambda i: (i, 0)), whole, whole],
        out_specs=pl.BlockSpec((bq, d), lambda i: (i, 0)),
        scratch_shapes=[pltpu.VMEM((dv, S), jnp.bfloat16), pltpu.VMEM((d, bq), jnp.bfloat16), pltpu.VMEM((2, max(bk, bq), qt), jnp.float32), pltpu.VMEM((dv, bq), jnp.float32),
                        pltpu.VMEM((1, bq), jnp.float32), pltpu.VMEM((1, bq), jnp.float32)],
        compiler_params=pltpu.CompilerParams(dimension_semantics=("arbitrary",), vmem_limit_bytes=60 * 2**20),
    )(q, k, v)


def solution(mesh):
    p = mesh.shape["seq"]
    n = math.isqrt(p // 2)
    rows = P(("data", "seq"), None)
    chunks, ahead = 8, 3

    def local(x, g, wqkv, wo):
        t, d = x.shape
        h, dh = wqkv.shape[2:]
        cos, sin = tables(n, t, dh, chunks)
        qkv = qkv_exchange(n, chunks, ahead, x, g, cos, sin, wqkv).reshape(3, p * t, dh)
        o = flash(qkv[0], qkv[1], qkv[2], 2048, 2048, 512, 256, 1, 1)
        o = lax.all_to_all(o.reshape(p, t, dh), "seq", 0, 0, tiled=True)
        o = o.reshape(n, n, 2, t, dh).transpose(3, 1, 0, 2, 4).reshape(t, h * dh)
        y = x.astype(F32) + jnp.dot(o, wo.reshape(h * dh, d), preferred_element_type=F32)
        return y.astype(x.dtype)

    return jax.shard_map(local, mesh=mesh,
                         in_specs=(rows, P(None), P(None, None, None, None), P(None, None, None)),
                         out_specs=rows, check_vma=False)
```

time: 555 us -> 233 us (0.42); the launches traced: 544 us -> 233 us
  matrix products: 212 us -> 17.5 us
  Pallas kernels: 0 us -> 169 us
  local copies, waits for them, and re-layouts: 156 us -> 9.62 us
  waiting for transfers between devices: 76.5 us -> 0 us
  other arithmetic: 49.5 us -> 3.31 us
  starting transfers between devices: 9.14 us -> 0 us
  blocking collectives: 40.6 us -> 33 us
    pallas_call x0 -> x2, Pallas kernels: none -> 169 us  [the longest x1 112 us: qkv_exchange(): pl.pallas_call(functools.partial(_qkv_kernel, n, nc, ahead), out_shape=ja...]
    dot_general x65 -> x1, matrix products: 174 us -> 17.5 us  [local(): jnp.dot(o, wo.reshape(h * dh, d), preferred_element_type=F32)]
    unnamed x72 -> x0, local copies, waits for them, and re-layouts: 138 us -> none
    all_to_all x1 -> x0, waiting for transfers between devices: 76.5 us -> none  [local(): buf = lax.all_to_all(buf, 'seq', 2, 1, tiled=True)]
    reduce_sum x33 -> x0, other arithmetic: 42.6 us -> none  [the longest x32 42.2 us: local(): pr = jax.nn.softmax(sc, axis=-1).astype(jnp.bfloat16)]
    unnamed x1 -> x0, matrix products: 38 us -> none
    all_to_all x1 -> x0, starting transfers between devices: 9.14 us -> none  [local(): buf = lax.all_to_all(buf, 'seq', 2, 1, tiled=True)]
    all_to_all x1 -> x0, local copies, waits for them, and re-layouts: 9.12 us -> none  [local(): buf = lax.all_to_all(buf, 'seq', 2, 1, tiled=True)]
  transfers between devices with their start and end apart: 1 -> 0, of which waited for: 1 -> 0; matrix products, arithmetic and copies ran while one was open for 0% -> 0% of each run, Pallas kernels for 0% -> 0%
where the time goes in v1:
time: 233 us
  Pallas kernels  169 us (73%)
  blocking collectives  33 us (14%)
  matrix products  17.5 us (8%)
  local copies, waits for them, and re-layouts  9.62 us (4%)
  other arithmetic  3.31 us (1%)
    pallas_call x1, Pallas kernels, qkv_exchange(): pl.pallas_call(functools.partial(_qkv_kernel, n, nc, ahead), out_shape=ja...  112 us
    pallas_call x1, Pallas kernels, flash(): pl.pallas_call(functools.partial(flash_kernel, bq=bq, bk=bk, qt=qt, sub=s...  57.6 us
    all_to_all x1, blocking collectives, local(): o = lax.all_to_all(o.reshape(p, t, dh), 'seq', 0, 0, tiled=True)  33 us
    dot_general x1, matrix products, local(): jnp.dot(o, wo.reshape(h * dh, d), preferred_element_type=F32)  17.5 us
    slice x1, local copies, waits for them, and re-layouts, local(): o = flash(qkv[0], qkv[1], qkv[2], 2048, 2048, 512, 256, 1, 1)  6.83 us

profile of v1, /device:TPU:97, one launch (start us, length us, event | category | flops | bytes accessed | tf_op | source)
XLA Modules:
  0.0 232.8 jit_solution(2657699614920904192)
XLA Ops:
  0.1 0.1 add_convert_fusion
  0.1 1.9 fusion.1
  2.0 1.3 pad_maximum_fusion
  3.4 111.7 %shard_map.46 = bf16[3,4,4,2,8,32,128]{6,5,4,3,2,1,0:T(8,128)(2,1)} custom-call(bf16[256,4096]{1,0:T(8,128)(2,1)} %x_ref.1, f32[1,4096]{1,0:T(1,128)} %bitcast.19, f32[4,8,32,128]{3,2,1,0:T(8,128)} %get-tuple-element.11.cos_ref, f32[4,8,32,128]{3,2,1,0:T(8,128)} %get-tuple-element.12.sin_ref, bf16[4096,3,32,128]{3,2,1,0:T(8,128)(2,1)} %w_ref.1), custom_call_target="tpu_custom_call" | custom-call | flops 25769803776 | bytes 41943040 | tf_op jit(solution)/shard_map/pallas_call | solution.py:204
  115.0 6.8 %fusion.2 = (bf16[1,4,4,2,8,32,128]{6,5,4,3,2,1,0:T(8,128)(2,1)}, bf16[1,4,4,2,8,32,128]{6,5,4,3,2,1,0:T(8,128)(2,1)}, bf16[1,4,4,2,8,32,128]{6,5,4,3,2,1,0:T(8,128)(2,1)}) fusion(bf16[3,4,4,2,8,32,128]{6,5,4,3,2,1,0:T(8,128)(2,1)} %shard_map.46), kind=kLoop, calls=%fused_computation.11 | loop fusion | bytes 12582912 | tf_op jit(solution)/shard_map/slice | solution.py:334
  121.9 57.6 %shard_map.47 = bf16[8192,128]{1,0:T(8,128)(2,1)} custom-call(bf16[8192,128]{1,0:T(8,128)(2,1)} %bitcast.18, bf16[8192,128]{1,0:T(8,128)(2,1)} %bitcast.17, bf16[8192,128]{1,0:T(8,128)(2,1)} %bitcast.16), custom_call_target="tpu_custom_call" | custom-call | tf_op jit(solution)/shard_map/pallas_call | solution.py:311
  179.4 33.0 %all_to_all.5 = bf16[32,256,128]{2,1,0:T(8,128)(2,1)} all-to-all(bf16[32,256,128]{2,1,0:T(8,128)(2,1)} %bitcast.15), channel_id=1, replica_groups=mesh['data'=1,'seq'=32] {'seq'}, dimensions={0} | all-to-all | bytes 4194304 | tf_op jit(solution)/shard_map/all_to_all | solution.py:335
  212.5 2.8 %copy.5 = bf16[256,4,4,2,128]{0,4,3,2,1:T(8,128)(2,1)S(1)} copy(bf16[256,4,4,2,128]{4,0,3,1,2:T(8,128)(2,1)} %bitcast.14) | data formatting | bytes 4194304 | tf_op jit(solution)/shard_map/transpose | solution.py:336
  215.3 17.5 %fusion = bf16[256,4096]{1,0:T(8,128)(2,1)} fusion(bf16[256,4096]{0,1:T(8,128)(2,1)S(1)} %bitcast.13, bf16[4096,4096]{1,0:T(8,128)(2,1)} %bitcast.12, bf16[256,4096]{1,0:T(8,128)(2,1)} %x_ref.1), kind=kOutput, calls=%fused_computation.1 | convolution fusion | flops 8593080320 | bytes 39845888 | tf_op jit(solution)/shard_map/dot_general | solution.py:337
  (3 shorter events, 0.0 us)

commit v2 on v1

v2 whole, which is shorter than its diff:
```python
import functools
import math

import jax
import jax.numpy as jnp
from jax import lax
from jax.experimental import pallas as pl
from jax.experimental.pallas import tpu as pltpu
from jax.sharding import PartitionSpec as P

BF = jnp.bfloat16
F32 = jnp.float32
MESH = pl.DeviceIdType.MESH


def _place(n):
    me = lax.axis_index("seq")
    core = lax.rem(me, 2)
    x = lax.rem(me // 2, n)
    y = me // (2 * n)
    return y, x, core, (lambda yy, xx, cc: {"seq": (yy * n + xx) * 2 + cc})


def _qkv_kernel(n, nc, ahead, x_ref, g_ref, cos_ref, sin_ref, w_ref, out_ref,
                xo, xg, wst, w, yo, yst, ro, rb, wsem, xs_s, xs_r, rl_s, ys_s, ys_r, rb_s, rb_r, fw_s, loc_s):
    t, d = x_ref.shape
    r = t // nc
    dk = wst.shape[1]
    y, x, core, dev = _place(n)
    way = 1 - 2 * core
    xf_, xb_ = lax.rem(x + way + n, n), lax.rem(x - way + n, n)
    yf_, yb_ = lax.rem(y + way + n, n), lax.rem(y - way + n, n)
    xslot = (xb_, xf_, lax.rem(x + 2, n))
    yd = [lax.rem(y + k, n) for k in range(n)]

    barrier = pltpu.get_barrier_semaphore()
    peers = [dev(y, xf_, core), dev(y, xb_, core), dev(y, x, 1 - core)]
    peers += [dev(yd[k], x, cc) for k in (1, n - 1) for cc in (0, 1)]
    for p_ in peers:
        pl.semaphore_signal(barrier, inc=1, device_id=p_, device_id_type=MESH)

    hb = x * (2 * n)
    nw = d // dk
    nb = wst.shape[0]

    def wload(i):
        return pltpu.make_async_copy(
            w_ref.at[pl.ds(pl.multiple_of(i * dk, dk), dk), :, pl.ds(pl.multiple_of(hb, 2 * n), 2 * n), :],
            wst.at[lax.rem(i, nb)], wsem.at[lax.rem(i, nb)])

    for i in range(nb):
        wload(i).start()

    def rows_of(j):
        return pl.ds(pl.multiple_of(j * r, r), r)

    def norm(j, _):
        xv = x_ref[rows_of(j), :].astype(F32)
        v = xv * lax.rsqrt(jnp.mean(xv * xv, axis=-1, keepdims=True) + 1e-5) * g_ref[...]
        xo[rows_of(j), :] = v.astype(BF)
        return 0

    def own(j, k):
        return pltpu.make_async_remote_copy(
            xo.at[rows_of(j), :], xg.at[j, k], xs_s.at[k, j], xs_r.at[k, j],
            device_id=dev(y, (xf_, xb_)[k], core), device_id_type=MESH)

    def relay(j):
        return pltpu.make_async_remote_copy(
            xg.at[j, 0], xg.at[j, 2], rl_s.at[j], xs_r.at[2, j],
            device_id=dev(y, xf_, core), device_id_type=MESH)

    lax.fori_loop(0, ahead, norm, 0)
    pl.semaphore_wait(barrier, len(peers))
    for j in range(ahead):
        own(j, 0).start()
        own(j, 1).start()
    lax.fori_loop(ahead, nc, norm, 0)
    sub = 32

    def relayout(i, _):
        wload(i).wait()
        slot = lax.rem(i, nb)
        for s in range(dk // sub):
            for c in range(3):
                vv = jnp.swapaxes(wst[slot, s * sub:(s + 1) * sub, c, :, :], 0, 1)
                for h in range(2 * n):
                    w[h // 2, pl.ds(pl.multiple_of(i * dk + s * sub, sub), sub),
                      ((h % 2) * 3 + c) * 128:((h % 2) * 3 + c + 1) * 128] = vv[h]

        @pl.when(i + nb < nw)
        def _():
            wload(i + nb).start()
        return 0

    lax.fori_loop(0, nw, relayout, 0)
    own(0, 0).wait_recv()
    relay(0).start()

    def at(whole, parts, j):
        return whole if j is None else parts.at[j]

    def sj(j):
        return nc if j is None else j

    def dst(yy, cc, j):
        return out_ref.at[:, yy, 0, cc] if j is None else out_ref.at[:, yy, pl.ds(1, 3), cc, rows_of(j)]

    def near(j, k, cc):
        return pltpu.make_async_remote_copy(
            at(yo, yst, j).at[k, cc], dst(y, core, j), ys_s.at[k, cc, sj(j)], ys_r.at[k, core, sj(j)],
            device_id=dev(yd[k], x, cc), device_id_type=MESH)

    def sibling(j):
        return pltpu.make_async_remote_copy(
            at(yo, yst, j).at[0, 1 - core], dst(y, core, j), ys_s.at[0, 1, sj(j)], ys_r.at[0, core, sj(j)],
            device_id=dev(y, x, 1 - core), device_id_type=MESH)

    def local(j):
        return pltpu.make_async_copy(at(yo, yst, j).at[0, core], dst(y, core, j), loc_s.at[sj(j)])

    def hop(j):
        return pltpu.make_async_remote_copy(
            at(yo, yst, j).at[2], at(ro, rb, j), rb_s.at[sj(j)], rb_r.at[sj(j)],
            device_id=dev(yf_, x, core), device_id_type=MESH)

    def forward(j, cc):
        return pltpu.make_async_remote_copy(
            at(ro, rb, j).at[cc], dst(yb_, core, j), fw_s.at[cc, sj(j)], ys_r.at[2, core, sj(j)],
            device_id=dev(yf_, x, cc), device_id_type=MESH)

    def pass_on(j):
        hop(j).wait_recv()
        forward(j, 0).start()
        forward(j, 1).start()

    def project(j, lhs, cosv, sinv, after_hop):
        for k in (2, 1, 3, 0):
            acc = jnp.dot(lhs, w[yd[k]], preferred_element_type=F32)
            for cc in range(2):
                for c in range(3):
                    v = acc[:, (cc * 3 + c) * 128:(cc * 3 + c + 1) * 128]
                    if c < 2:
                        v = v * cosv + pltpu.roll(v, 64, 1) * sinv
                    v = v.astype(BF)
                    if j is None:
                        yo[k, cc, c] = v
                    else:
                        yst[j, k, cc, c] = v.reshape(3, r, 128)
            if k == 2:
                hop(j).start()
                after_hop()
            elif k == 0:
                sibling(j).start()
                local(j).start()
            else:
                near(j, k, 0).start()
                near(j, k, 1).start()

    project(None, xo[...], cos_ref[x].reshape(t, 128), sin_ref[x].reshape(t, 128), lambda: None)

    def step(j, _):
        @pl.when(j + ahead < nc)
        def _():
            own(j + ahead, 0).start()
            own(j + ahead, 1).start()

        @pl.when(j + 1 < nc)
        def _():
            own(j + 1, 0).wait_recv()
            relay(j + 1).start()

        own(j, 1).wait_recv()
        relay(j).wait_recv()
        lhs = xg[j].reshape(3 * r, d)
        cosv = jnp.concatenate([cos_ref[xs, j] for xs in xslot], axis=0)
        sinv = jnp.concatenate([sin_ref[xs, j] for xs in xslot], axis=0)

        def after_hop():
            @pl.when(j == 0)
            def _():
                pass_on(None)

            @pl.when(j > 0)
            def _():
                pass_on(j - 1)

        project(j, lhs, cosv, sinv, after_hop)
        return 0

    lax.fori_loop(0, nc, step, 0)
    pass_on(nc - 1)

    def finish(j):
        hop(j).wait_send()
        for cc in range(2):
            forward(j, cc).wait_send()
            for k in (1, 3):
                near(j, k, cc).wait_send()
        sibling(j).wait_send()
        local(j).wait()
        for k in (1, 2, 3):
            for cc in range(2):
                pltpu.make_async_remote_copy(
                    at(yo, yst, j).at[k, cc], dst(yd[n - k], cc, j), ys_s.at[k, cc, sj(j)], ys_r.at[k, cc, sj(j)],
                    device_id=dev(y, x, 1 - core), device_id_type=MESH).wait_recv()
        pltpu.make_async_remote_copy(
            at(yo, yst, j).at[0, core], dst(y, 1 - core, j), ys_s.at[0, 1, sj(j)], ys_r.at[0, 1 - core, sj(j)],
            device_id=dev(y, x, 1 - core), device_id_type=MESH).wait_recv()

    finish(None)

    def drain(j, _):
        for k in range(2):
            own(j, k).wait_send()
        relay(j).wait_send()
        finish(j)
        return 0

    lax.fori_loop(0, nc, drain, 0)


def qkv_exchange(n, nc, ahead, x, g, cos, sin, wqkv):
    t, d = x.shape
    h, dh = wqkv.shape[2:]
    r = t // nc
    dk = 128
    vm = pl.BlockSpec(memory_space=pltpu.VMEM)
    dma = pltpu.SemaphoreType.DMA
    return pl.pallas_call(
        functools.partial(_qkv_kernel, n, nc, ahead),
        out_shape=jax.ShapeDtypeStruct((3, n, 4, 2, t, dh), BF),
        in_specs=[vm, vm, vm, vm, pl.BlockSpec(memory_space=pl.ANY)],
        out_specs=pl.BlockSpec(memory_space=pl.ANY),
        scratch_shapes=[
            pltpu.VMEM((t, d), BF),
            pltpu.VMEM((nc, 3, r, d), BF),
            pltpu.VMEM((6, dk, 3, 2 * n, dh), BF),
            pltpu.VMEM((n, d, 6 * dh), BF),
            pltpu.VMEM((n, 2, 3, t, dh), BF),
            pltpu.VMEM((nc, n, 2, 3, 3, r, dh), BF),
            pltpu.VMEM((2, 3, t, dh), BF),
            pltpu.VMEM((nc, 2, 3, 3, r, dh), BF),
            dma((6,)), dma((2, nc)), dma((3, nc)), dma((nc,)),
            dma((n, 2, nc + 1)), dma((n, 2, nc + 1)), dma((nc + 1,)), dma((nc + 1,)), dma((2, nc + 1)), dma((nc + 1,)),
        ],
        compiler_params=pltpu.CompilerParams(collective_id=0, has_side_effects=True, vmem_limit_bytes=64 * 2**20 - 2**16),
        cost_estimate=pl.CostEstimate(flops=2 * t * d * 3 * h * dh, bytes_accessed=40 * 2**20, transcendentals=0),
    )(x, g.reshape(1, d), cos, sin, wqkv)


def tables(n, t, dh, nc):
    y, x, core, _ = _place(n)
    pos = (((y * n + jnp.arange(n))[:, None] * 2 + core) * t + jnp.arange(t)[None, :]).astype(F32)
    inv = 10000.0 ** (-jnp.arange(dh // 2, dtype=F32) * 2.0 / dh)
    ang = pos[..., None] * inv
    cos, sin = jnp.cos(ang), jnp.sin(ang)
    shape = (n, nc, t // nc, dh)
    return jnp.concatenate([cos, cos], -1).reshape(shape), jnp.concatenate([-sin, sin], -1).reshape(shape)


NEG = -1e30


def _attn_kernel(n, qt, bk, sub, qkv_ref, x_ref, wo_ref, y_ref,
                 qkv, xv, wo, ob, acc, yacc, vt, qtr, sa, sb, m, ma, mb, insem, wosem, osem, rsem):
    q, k, v = qkv.at[0], qkv.at[1], qkv.at[2]
    s_len, d = k.shape
    t = ob.shape[0]
    dv = vt.shape[0]
    p = s_len // t
    groups = s_len // qt
    per = qt // t
    c = (d ** -0.5) * math.log2(math.e)
    me = lax.axis_index("seq")
    y, x, core, _ = _place(n)
    head = (x * n + y) * 2 + core
    rot = head // (p // groups)
    my_tile = me // per

    def dev_head(h):
        return (lax.rem(h // 2, n) * n + h // (2 * n)) * 2 + lax.rem(h, 2)

    barrier = pltpu.get_barrier_semaphore()

    def greet(i, _):
        pl.semaphore_signal(barrier, inc=1, device_id={"seq": lax.rem(me + i, p)}, device_id_type=MESH)
        return 0

    lax.fori_loop(1, p, greet, 0)
    for yy in range(n):
        for slot in range(4):
            for cc in range(2):
                off = (0, 2 * cc - 1, 1 - 2 * cc, 2)[slot]
                row = ((yy * n + lax.rem(x + off + n, n)) * 2 + cc) * t
                pltpu.make_async_copy(qkv_ref.at[:, yy, slot, cc], qkv.at[:, pl.ds(pl.multiple_of(row, t), t), :],
                                      insem.at[0]).start()
    pltpu.make_async_copy(x_ref, xv, insem.at[1]).start()
    kw = wo.shape[0] // groups

    def wload(g):
        rows = pl.ds(pl.multiple_of(g * kw, kw), kw)
        return pltpu.make_async_copy(wo_ref.at[rows, :], wo.at[rows, :], wosem.at[g])

    for g in range(groups):
        wload(g).start()
    vt[d:, :] = jnp.ones((dv - d, s_len), BF)
    pltpu.make_async_copy(qkv, qkv, insem.at[0]).wait()

    def tr(j, _):
        blk = pl.ds(pl.multiple_of(j * 512, 512), 512)
        vt[0:d, blk] = v[blk, :].T
        return 0

    lax.fori_loop(0, s_len // 512, tr, 0)

    def qk(j, s_ref, mm, bias=None):
        mx = None
        qv = qtr[...]
        for u in range(bk // sub):
            ks = pl.ds(pl.multiple_of(j * bk + u * sub, sub), sub)
            s = jnp.dot(k[ks, :], qv, preferred_element_type=F32)
            if bias is not None:
                kp = lax.broadcasted_iota(jnp.int32, s.shape, 0) + u * sub
                qp = lax.broadcasted_iota(jnp.int32, s.shape, 1)
                s = jnp.where(kp - qp <= bias, s, NEG)
            s_ref[u * sub:(u + 1) * sub, :] = s
            sm = jnp.max(s, axis=0, keepdims=True)
            mx = sm if mx is None else jnp.maximum(mx, sm)
        mm[...] = mx

    def pv(j, s_ref, mm):
        m_old = m[...]
        m_new = jnp.maximum(m_old, mm[...])
        a = jnp.exp2((m_old - m_new) * c)
        mc = m_new * c
        part = None
        for u in range(bk // sub):
            ks = pl.ds(pl.multiple_of(j * bk + u * sub, sub), sub)
            pr = jnp.exp2(s_ref[u * sub:(u + 1) * sub, :] * c - mc)
            dd = jnp.dot(vt[:, ks], pr.astype(BF), preferred_element_type=F32)
            part = dd if part is None else part + dd
        m[...] = m_new
        acc[...] = acc[...] * a + part

    def send(tile, e):
        to = tile * per + e
        return pltpu.make_async_remote_copy(
            v.at[pl.ds(pl.multiple_of(tile * qt + e * t, t), t), :], ob.at[:, pl.ds(pl.multiple_of(head * d, d), d)],
            osem.at[tile, e], rsem.at[head], device_id={"seq": to}, device_id_type=MESH)

    def keep(tile, e):
        return pltpu.make_async_copy(
            v.at[pl.ds(pl.multiple_of(tile * qt + e * t, t), t), :], ob.at[:, pl.ds(pl.multiple_of(head * d, d), d)], osem.at[tile, e])

    def tile_body(i, _):
        tile = lax.rem(i + rot, groups)
        rows = pl.ds(pl.multiple_of(tile * qt, qt), qt)
        qtr[...] = q[rows, :].T
        acc[...] = jnp.zeros_like(acc)
        m[...] = jnp.full_like(m, NEG)
        last = (tile * qt) // bk
        bias = tile * qt - last * bk

        @pl.when(last == 0)
        def _():
            qk(0, sa, ma, bias)
            pv(0, sa, ma)

        @pl.when(last > 0)
        def _():
            qk(0, sa, ma)

            def pair(jj, _):
                qk(2 * jj + 1, sb, mb)
                pv(2 * jj, sa, ma)
                qk(2 * jj + 2, sa, ma)
                pv(2 * jj + 1, sb, mb)
                return 0

            npair = (last - 1) // 2
            lax.fori_loop(0, npair, pair, 0)
            b0 = 2 * npair

            @pl.when(last - b0 == 1)
            def _():
                qk(last, sb, mb, bias)
                pv(b0, sa, ma)
                pv(last, sb, mb)

            @pl.when(last - b0 == 2)
            def _():
                qk(b0 + 1, sb, mb)
                pv(b0, sa, ma)
                qk(last, sa, ma, bias)
                pv(b0 + 1, sb, mb)
                pv(last, sa, ma)

        o = acc[0:d, :] * (1.0 / acc[d:d + 1, :])
        v[rows, :] = o.T.astype(BF)

        @pl.when(i == 0)
        def _():
            pl.semaphore_wait(barrier, p - 1)

        for e in range(per):
            @pl.when(tile * per + e == me)
            def _():
                keep(tile, e).start()

            @pl.when(tile * per + e != me)
            def _():
                send(tile, e).start()
        return 0

    lax.fori_loop(0, groups, tile_body, 0)
    pltpu.make_async_copy(x_ref, xv, insem.at[1]).wait()
    hp = p // groups
    cw = 1024

    def arrive(h):
        @pl.when(h == head)
        def _():
            keep(my_tile, lax.rem(me, per)).wait()

        @pl.when(h != head)
        def _():
            pltpu.make_async_remote_copy(
                v.at[pl.ds(0, t), :], ob.at[:, pl.ds(pl.multiple_of(h * d, d), d)],
                osem.at[0, 0], rsem.at[h], device_id={"seq": dev_head(h)}, device_id_type=MESH).wait_recv()

    def project(i, _):
        g = lax.rem(my_tile - i + groups, groups)
        wload(g).wait()
        for e in range(hp):
            arrive(g * hp + e)
        o = ob[:, pl.ds(pl.multiple_of(g * kw, kw), kw)]

        def cols(j, _):
            cs = pl.ds(pl.multiple_of(j * cw, cw), cw)
            dd = jnp.dot(o, wo[pl.ds(pl.multiple_of(g * kw, kw), kw), cs], preferred_element_type=F32)

            @pl.when(i == 0)
            def _():
                yacc[:, cs] = xv[:, cs].astype(F32) + dd

            @pl.when(jnp.logical_and(i > 0, i < groups - 1))
            def _():
                yacc[:, cs] = yacc[:, cs] + dd

            @pl.when(i == groups - 1)
            def _():
                y_ref[:, cs] = (yacc[:, cs] + dd).astype(BF)
            return 0

        lax.fori_loop(0, wo.shape[1] // cw, cols, 0)
        return 0

    lax.fori_loop(0, groups, project, 0)

    def drain(tile, _):
        for e in range(per):
            @pl.when(tile * per + e != me)
            def _():
                send(tile, e).wait_send()
        return 0

    lax.fori_loop(0, groups, drain, 0)


def attend(n, qt, bk, sub, qkv, x, wo):
    t, dm = x.shape
    hd = wo.shape[0]
    d = qkv.shape[-1]
    p = 2 * n * n
    s_len = p * t
    groups = s_len // qt
    any_ = pl.BlockSpec(memory_space=pl.ANY)
    dma = pltpu.SemaphoreType.DMA

    return pl.pallas_call(
        functools.partial(_attn_kernel, n, qt, bk, sub),
        out_shape=jax.ShapeDtypeStruct((t, dm), BF),
        in_specs=[any_, any_, any_],
        out_specs=pl.BlockSpec(memory_space=pltpu.VMEM),
        scratch_shapes=[
            pltpu.VMEM((3, s_len, d), BF),
            pltpu.VMEM((t, dm), BF), pltpu.VMEM((hd, dm), BF), pltpu.VMEM((t, hd), BF),
            pltpu.VMEM((d + 16, qt), F32), pltpu.VMEM((t, dm), F32),
            pltpu.VMEM((d + 16, s_len), BF), pltpu.VMEM((d, qt), BF),
            pltpu.VMEM((bk, qt), F32), pltpu.VMEM((bk, qt), F32),
            pltpu.VMEM((1, qt), F32), pltpu.VMEM((1, qt), F32), pltpu.VMEM((1, qt), F32),
            dma((4,)), dma((groups,)), dma((groups, qt // t)), dma((p,)),
        ],
        compiler_params=pltpu.CompilerParams(collective_id=1, has_side_effects=True, vmem_limit_bytes=64 * 2**20 - 2**16),
        cost_estimate=pl.CostEstimate(flops=2 * s_len * s_len * d + 2 * t * hd * dm, bytes_accessed=2 * hd * dm, transcendentals=s_len * s_len // 2),
    )(qkv, x, wo)


def solution(mesh):
    p = mesh.shape["seq"]
    n = math.isqrt(p // 2)
    rows = P(("data", "seq"), None)
    chunks, ahead = 8, 3

    def local(x, g, wqkv, wo):
        t, d = x.shape
        h, dh = wqkv.shape[2:]
        cos, sin = tables(n, t, dh, chunks)
        qkv = qkv_exchange(n, chunks, ahead, x, g, cos, sin, wqkv)
        return attend(n, 1024, 1024, 512, qkv, x, wo.reshape(h * dh, d))

    return jax.shard_map(local, mesh=mesh,
                         in_specs=(rows, P(None), P(None, None, None, None), P(None, None, None)),
                         out_specs=rows, check_vma=False)
```

time: 233 us -> 190 us (0.82)
  blocking collectives: 33 us -> 0 us
  matrix products: 17.5 us -> 0 us
  Pallas kernels: 169 us -> 184 us
  local copies, waits for them, and re-layouts: 9.62 us -> 3.13 us
    all_to_all x1 -> x0, blocking collectives: 33 us -> none  [local(): o = lax.all_to_all(o.reshape(p, t, dh), 'seq', 0, 0, tiled=True)]
    pallas_call x1, Pallas kernels: 57.6 us -> 84.1 us  [attend(): pl.pallas_call(functools.partial(_attn_kernel, n, qt, bk, sub), out_shape...]
    dot_general x1 -> x0, matrix products: 17.5 us -> none  [local(): jnp.dot(o, wo.reshape(h * dh, d), preferred_element_type=F32)]
    pallas_call x1, Pallas kernels: 112 us -> 99.4 us  [qkv_exchange(): pl.pallas_call(functools.partial(_qkv_kernel, n, nc, ahead), out_shape=ja...]
    slice x1 -> x0, local copies, waits for them, and re-layouts: 6.83 us -> none  [local(): o = flash(qkv[0], qkv[1], qkv[2], 2048, 2048, 512, 256, 1, 1)]
    unnamed x0 -> x1, local copies, waits for them, and re-layouts: none -> 3.13 us
    transpose x1 -> x0, local copies, waits for them, and re-layouts: 2.79 us -> none  [local(): o = o.reshape(n, n, 2, t, dh).transpose(3, 1, 0, 2, 4).reshape(t, h * dh)]
where the time goes in v2:
time: 190 us
  Pallas kernels  184 us (97%)
  other arithmetic  3.31 us (2%)
  local copies, waits for them, and re-layouts  3.13 us (2%)
    pallas_call x1, Pallas kernels, qkv_exchange(): pl.pallas_call(functools.partial(_qkv_kernel, n, nc, ahead), out_shape=ja...  99.4 us
    pallas_call x1, Pallas kernels, attend(): pl.pallas_call(functools.partial(_attn_kernel, n, qt, bk, sub), out_shape...  84.1 us

profile of v2, /device:TPU:97, one launch (start us, length us, event | category | flops | bytes accessed | tf_op | source)
XLA Modules:
  0.0 190.0 jit_solution(7842618008272791412)
XLA Ops:
  0.0 0.1 add_convert_fusion
  0.1 1.9 %fusion = (f32[4,8,32,64]{3,2,1,0:T(8,128)S(1)}, f32[4,8,32,64]{3,2,1,0:T(8,128)S(1)}, f32[4,8,32,64]{3,2,1,0:T(8,128)S(1)}) fusion(f32[64]{0:T(128)S(1)} %multiply_power_fusion, f32[4,8,32]{2,1,0:T(8,128)S(1)} %add_convert_fusion), kind=kLoop, calls=%fused_computation.4 | loop fusion | flops 131072 | bytes 790784 | tf_op jit(solution)/shard_map/neg | solution.py:259
  2.0 1.3 pad_maximum_fusion
  3.3 99.4 %shard_map.46.qkv_ref = bf16[3,4,4,2,256,128]{5,4,3,2,1,0:T(8,128)(2,1)} custom-call(bf16[256,4096]{1,0:T(8,128)(2,1)} %x_ref.3, f32[1,4096]{1,0:T(1,128)} %bitcast.2, f32[4,8,32,128]{3,2,1,0:T(8,128)} %get-tuple-element.8.cos_ref, f32[4,8,32,128]{3,2,1,0:T(8,128)} %get-tuple-element.9.sin_ref, bf16[4096,3,32,128]{3,2,1,0:T(8,128)(2,1)} %w_ref.1), custom_call_target="tpu_custom_call" | custom-call | flops 25769803776 | bytes 41943040 | tf_op jit(solution)/shard_map/pallas_call | solution.py:230
  102.8 84.1 %shard_map.47 = bf16[256,4096]{1,0:T(8,128)(2,1)} custom-call(bf16[3,4,4,2,256,128]{5,4,3,2,1,0:T(8,128)(2,1)} %shard_map.46.qkv_ref, bf16[256,4096]{1,0:T(8,128)(2,1)} %x_ref.3, bf16[4096,4096]{1,0:T(8,128)(2,1)} %bitcast.3), custom_call_target="tpu_custom_call" | custom-call | flops 25769803776 | bytes 33554432 | tf_op jit(solution)/shard_map/pallas_call | solution.py:481
  186.9 3.1 %copy.6 = bf16[256,4096]{1,0:T(8,128)(2,1)} copy(bf16[256,4096]{1,0:T(8,128)(2,1)} %shard_map.47) | data formatting | bytes 4194304
  (3 shorter events, 0.0 us)

commit v3 on v2

--- a/solution.py
+++ b/solution.py
@@ -21,7 +21,7 @@
     return y, x, core, (lambda yy, xx, cc: {"seq": (yy * n + xx) * 2 + cc})
 
 
-def _qkv_kernel(n, nc, ahead, x_ref, g_ref, cos_ref, sin_ref, w_ref, out_ref,
+def _qkv_kernel(n, nc, ahead, x_ref, g_ref, inv_ref, w_ref, out_ref,
                 xo, xg, wst, w, yo, yst, ro, rb, wsem, xs_s, xs_r, rl_s, ys_s, ys_r, rb_s, rb_r, fw_s, loc_s):
     t, d = x_ref.shape
     r = t // nc
@@ -53,6 +53,13 @@
 
     def rows_of(j):
         return pl.ds(pl.multiple_of(j * r, r), r)
+
+    def turn(xs, first, rows):
+        pos = lax.broadcasted_iota(jnp.int32, (rows, 128), 0) + (((y * n + xs) * 2 + core) * t + first)
+        ang = pos.astype(F32) * inv_ref[...]
+        low = lax.broadcasted_iota(jnp.int32, (rows, 128), 1) < 64
+        s = jnp.sin(ang)
+        return jnp.cos(ang), jnp.where(low, -s, s)
 
     def norm(j, _):
         xv = x_ref[rows_of(j), :].astype(F32)
@@ -149,32 +156,36 @@
                         yst[j, k, cc, c] = v.reshape(3, r, 128)
             if k == 2:
                 hop(j).start()
+            if k == 1:
+                near(j, 1, 0).start()
+                near(j, 1, 1).start()
                 after_hop()
             elif k == 0:
                 sibling(j).start()
                 local(j).start()
-            else:
+            elif k == 3:
                 near(j, k, 0).start()
                 near(j, k, 1).start()
 
-    project(None, xo[...], cos_ref[x].reshape(t, 128), sin_ref[x].reshape(t, 128), lambda: None)
+    project(None, xo[...], *turn(x, 0, t), lambda: None)
 
     def step(j, _):
+        @pl.when(j + 1 < nc)
+        def _():
+            own(j + 1, 0).wait_recv()
+            relay(j + 1).start()
+
         @pl.when(j + ahead < nc)
         def _():
             own(j + ahead, 0).start()
             own(j + ahead, 1).start()
 
-        @pl.when(j + 1 < nc)
-        def _():
-            own(j + 1, 0).wait_recv()
-            relay(j + 1).start()
-
+        cs = [turn(xs, j * r, r) for xs in xslot]
+        cosv = jnp.concatenate([u[0] for u in cs], axis=0)
+        sinv = jnp.concatenate([u[1] for u in cs], axis=0)
         own(j, 1).wait_recv()
         relay(j).wait_recv()
         lhs = xg[j].reshape(3 * r, d)
-        cosv = jnp.concatenate([cos_ref[xs, j] for xs in xslot], axis=0)
-        sinv = jnp.concatenate([sin_ref[xs, j] for xs in xslot], axis=0)
 
         def after_hop():
             @pl.when(j == 0)
@@ -220,17 +231,19 @@
     lax.fori_loop(0, nc, drain, 0)
 
 
-def qkv_exchange(n, nc, ahead, x, g, cos, sin, wqkv):
+def qkv_exchange(n, nc, ahead, x, g, wqkv):
     t, d = x.shape
     h, dh = wqkv.shape[2:]
     r = t // nc
     dk = 128
+    inv = 10000.0 ** (-jnp.arange(dh // 2, dtype=F32) * 2.0 / dh)
+    inv = jnp.concatenate([inv, inv]).reshape(1, dh)
     vm = pl.BlockSpec(memory_space=pltpu.VMEM)
     dma = pltpu.SemaphoreType.DMA
     return pl.pallas_call(
         functools.partial(_qkv_kernel, n, nc, ahead),
         out_shape=jax.ShapeDtypeStruct((3, n, 4, 2, t, dh), BF),
-        in_specs=[vm, vm, vm, vm, pl.BlockSpec(memory_space=pl.ANY)],
+        in_specs=[vm, vm, vm, pl.BlockSpec(memory_space=pl.ANY)],
         out_specs=pl.BlockSpec(memory_space=pl.ANY),
         scratch_shapes=[
             pltpu.VMEM((t, d), BF),
@@ -246,26 +259,17 @@
         ],
         compiler_params=pltpu.CompilerParams(collective_id=0, has_side_effects=True, vmem_limit_bytes=64 * 2**20 - 2**16),
         cost_estimate=pl.CostEstimate(flops=2 * t * d * 3 * h * dh, bytes_accessed=40 * 2**20, transcendentals=0),
-    )(x, g.reshape(1, d), cos, sin, wqkv)
-
-
-def tables(n, t, dh, nc):
-    y, x, core, _ = _place(n)
-    pos = (((y * n + jnp.arange(n))[:, None] * 2 + core) * t + jnp.arange(t)[None, :]).astype(F32)
-    inv = 10000.0 ** (-jnp.arange(dh // 2, dtype=F32) * 2.0 / dh)
-    ang = pos[..., None] * inv
-    cos, sin = jnp.cos(ang), jnp.sin(ang)
-    shape = (n, nc, t // nc, dh)
-    return jnp.concatenate([cos, cos], -1).reshape(shape), jnp.concatenate([-sin, sin], -1).reshape(shape)
+    )(x, g.reshape(1, d), inv, wqkv)
 
 
 NEG = -1e30
 
 
-def _attn_kernel(n, qt, bk, sub, qkv_ref, x_ref, wo_ref, y_ref,
+def _attn_kernel(n, qt, sub, cw, psub, qkv_ref, x_ref, wo_ref, y_ref,
                  qkv, xv, wo, ob, acc, yacc, vt, qtr, sa, sb, m, ma, mb, insem, wosem, osem, rsem):
     q, k, v = qkv.at[0], qkv.at[1], qkv.at[2]
     s_len, d = k.shape
+    bk = qt
     t = ob.shape[0]
     dv = vt.shape[0]
     p = s_len // t
@@ -314,34 +318,39 @@
 
     lax.fori_loop(0, s_len // 512, tr, 0)
 
-    def qk(j, s_ref, mm, bias=None):
-        mx = None
-        qv = qtr[...]
+    def qk(j, s_ref, mm, diag=False):
+        mx = [None] * (qt // cw)
         for u in range(bk // sub):
             ks = pl.ds(pl.multiple_of(j * bk + u * sub, sub), sub)
-            s = jnp.dot(k[ks, :], qv, preferred_element_type=F32)
-            if bias is not None:
-                kp = lax.broadcasted_iota(jnp.int32, s.shape, 0) + u * sub
-                qp = lax.broadcasted_iota(jnp.int32, s.shape, 1)
-                s = jnp.where(kp - qp <= bias, s, NEG)
-            s_ref[u * sub:(u + 1) * sub, :] = s
-            sm = jnp.max(s, axis=0, keepdims=True)
-            mx = sm if mx is None else jnp.maximum(mx, sm)
-        mm[...] = mx
-
-    def pv(j, s_ref, mm):
-        m_old = m[...]
-        m_new = jnp.maximum(m_old, mm[...])
-        a = jnp.exp2((m_old - m_new) * c)
-        mc = m_new * c
-        part = None
-        for u in range(bk // sub):
-            ks = pl.ds(pl.multiple_of(j * bk + u * sub, sub), sub)
-            pr = jnp.exp2(s_ref[u * sub:(u + 1) * sub, :] * c - mc)
-            dd = jnp.dot(vt[:, ks], pr.astype(BF), preferred_element_type=F32)
-            part = dd if part is None else part + dd
-        m[...] = m_new
-        acc[...] = acc[...] * a + part
+            c0 = (u * sub) // cw * cw if diag else 0
+            s = jnp.dot(k[ks, :], qtr[:, c0:], preferred_element_type=F32)
+            for h in range(c0 // cw, qt // cw):
+                sh = s[:, h * cw - c0:(h + 1) * cw - c0]
+                if diag and u * sub + sub > h * cw:
+                    kp = lax.broadcasted_iota(jnp.int32, sh.shape, 0) + u * sub
+                    qp = lax.broadcasted_iota(jnp.int32, sh.shape, 1) + h * cw
+                    sh = jnp.where(kp <= qp, sh, NEG)
+                s_ref[u * sub:(u + 1) * sub, h * cw:(h + 1) * cw] = sh
+                sm = jnp.max(sh, axis=0, keepdims=True)
+                mx[h] = sm if mx[h] is None else jnp.maximum(mx[h], sm)
+        for h in range(qt // cw):
+            mm[:, h * cw:(h + 1) * cw] = mx[h]
+
+    def pv(j, s_ref, mm, diag=False):
+        for h in range(qt // cw):
+            cols = slice(h * cw, (h + 1) * cw)
+            m_old = m[:, cols]
+            m_new = jnp.maximum(m_old, mm[:, cols])
+            a = jnp.exp2((m_old - m_new) * c)
+            mc = m_new * c
+            part = None
+            for u in range(((h + 1) * cw if diag else bk) // psub):
+                ks = pl.ds(pl.multiple_of(j * bk + u * psub, psub), psub)
+                pr = jnp.exp2(s_ref[u * psub:(u + 1) * psub, cols] * c - mc)
+                dd = jnp.dot(vt[:, ks], pr.astype(BF), preferred_element_type=F32)
+                part = dd if part is None else part + dd
+            m[:, cols] = m_new
+            acc[:, cols] = acc[:, cols] * a + part
 
     def send(tile, e):
         to = tile * per + e
@@ -359,13 +368,12 @@
         qtr[...] = q[rows, :].T
         acc[...] = jnp.zeros_like(acc)
         m[...] = jnp.full_like(m, NEG)
-        last = (tile * qt) // bk
-        bias = tile * qt - last * bk
+        last = tile
 
         @pl.when(last == 0)
         def _():
-            qk(0, sa, ma, bias)
-            pv(0, sa, ma)
+            qk(0, sa, ma, True)
+            pv(0, sa, ma, True)
 
         @pl.when(last > 0)
         def _():
@@ -384,17 +392,17 @@
 
             @pl.when(last - b0 == 1)
             def _():
-                qk(last, sb, mb, bias)
+                qk(last, sb, mb, True)
                 pv(b0, sa, ma)
-                pv(last, sb, mb)
+                pv(last, sb, mb, True)
 
             @pl.when(last - b0 == 2)
             def _():
                 qk(b0 + 1, sb, mb)
                 pv(b0, sa, ma)
-                qk(last, sa, ma, bias)
+                qk(last, sa, ma, True)
                 pv(b0 + 1, sb, mb)
-                pv(last, sa, ma)
+                pv(last, sa, ma, True)
 
         o = acc[0:d, :] * (1.0 / acc[d:d + 1, :])
         v[rows, :] = o.T.astype(BF)
@@ -468,7 +476,7 @@
     lax.fori_loop(0, groups, drain, 0)
 
 
-def attend(n, qt, bk, sub, qkv, x, wo):
+def attend(n, qt, sub, cw, psub, qkv, x, wo):
     t, dm = x.shape
     hd = wo.shape[0]
     d = qkv.shape[-1]
@@ -479,7 +487,7 @@
     dma = pltpu.SemaphoreType.DMA
 
     return pl.pallas_call(
-        functools.partial(_attn_kernel, n, qt, bk, sub),
+        functools.partial(_attn_kernel, n, qt, sub, cw, psub),
         out_shape=jax.ShapeDtypeStruct((t, dm), BF),
         in_specs=[any_, any_, any_],
         out_specs=pl.BlockSpec(memory_space=pltpu.VMEM),
@@ -488,7 +496,7 @@
             pltpu.VMEM((t, dm), BF), pltpu.VMEM((hd, dm), BF), pltpu.VMEM((t, hd), BF),
             pltpu.VMEM((d + 16, qt), F32), pltpu.VMEM((t, dm), F32),
             pltpu.VMEM((d + 16, s_len), BF), pltpu.VMEM((d, qt), BF),
-            pltpu.VMEM((bk, qt), F32), pltpu.VMEM((bk, qt), F32),
+            pltpu.VMEM((qt, qt), F32), pltpu.VMEM((qt, qt), F32),
             pltpu.VMEM((1, qt), F32), pltpu.VMEM((1, qt), F32), pltpu.VMEM((1, qt), F32),
             dma((4,)), dma((groups,)), dma((groups, qt // t)), dma((p,)),
         ],
@@ -506,9 +514,8 @@
     def local(x, g, wqkv, wo):
         t, d = x.shape
         h, dh = wqkv.shape[2:]
-        cos, sin = tables(n, t, dh, chunks)
-        qkv = qkv_exchange(n, chunks, ahead, x, g, cos, sin, wqkv)
-        return attend(n, 1024, 1024, 512, qkv, x, wo.reshape(h * dh, d))
+        qkv = qkv_exchange(n, chunks, ahead, x, g, wqkv)
+        return attend(n, 1024, 512, 256, 256, qkv, x, wo.reshape(h * dh, d))
 
     return jax.shard_map(local, mesh=mesh,
                          in_specs=(rows, P(None), P(None, None, None, None), P(None, None, None)),

time: 190 us -> 179 us (0.942)
  Pallas kernels: 184 us -> 175 us
  other arithmetic: 3.31 us -> 0.6 us
    pallas_call x1, Pallas kernels: 84.1 us -> 79.4 us  [attend(): pl.pallas_call(functools.partial(_attn_kernel, n, qt, sub, cw, psub), out...]
    pallas_call x1, Pallas kernels: 99.4 us -> 95.8 us  [qkv_exchange(): pl.pallas_call(functools.partial(_qkv_kernel, n, nc, ahead), out_shape=ja...]
    neg x1 -> x0, other arithmetic: 1.91 us -> none  [tables(): -sin]
where the time goes in v3:
time: 179 us
  Pallas kernels  175 us (98%)
  local copies, waits for them, and re-layouts  3.13 us (2%)
    pallas_call x1, Pallas kernels, qkv_exchange(): pl.pallas_call(functools.partial(_qkv_kernel, n, nc, ahead), out_shape=ja...  95.8 us
    pallas_call x1, Pallas kernels, attend(): pl.pallas_call(functools.partial(_attn_kernel, n, qt, sub, cw, psub), out...  79.4 us

profile of v3, /device:TPU:97, one launch (start us, length us, event | category | flops | bytes accessed | tf_op | source)
XLA Modules:
  0.0 179.0 jit_solution(11797954904068025738)
XLA Ops:
  0.0 0.6 maximum_bitcast_fusion.inv_ref
  0.6 95.8 %shard_map.46.qkv_ref = bf16[3,4,4,2,256,128]{5,4,3,2,1,0:T(8,128)(2,1)} custom-call(bf16[256,4096]{1,0:T(8,128)(2,1)} %x_ref.3, f32[1,4096]{1,0:T(1,128)} %bitcast.4, f32[1,128]{1,0:T(1,128)} %maximum_bitcast_fusion.inv_ref, bf16[4096,3,32,128]{3,2,1,0:T(8,128)(2,1)} %w_ref.1), custom_call_target="tpu_custom_call" | custom-call | flops 25769803776 | bytes 41943040 | tf_op jit(solution)/shard_map/pallas_call | solution.py:243
  96.4 79.4 %shard_map.47 = bf16[256,4096]{1,0:T(8,128)(2,1)} custom-call(bf16[3,4,4,2,256,128]{5,4,3,2,1,0:T(8,128)(2,1)} %shard_map.46.qkv_ref, bf16[256,4096]{1,0:T(8,128)(2,1)} %x_ref.3, bf16[4096,4096]{1,0:T(8,128)(2,1)} %bitcast.5), custom_call_target="tpu_custom_call" | custom-call | flops 25769803776 | bytes 33554432 | tf_op jit(solution)/shard_map/pallas_call | solution.py:489
  175.9 3.1 %copy.6 = bf16[256,4096]{1,0:T(8,128)(2,1)} copy(bf16[256,4096]{1,0:T(8,128)(2,1)} %shard_map.47) | data formatting | bytes 4194304
  (1 shorter events, 0.0 us)
